TPU v7x, 32 devices: a whole 2x2x4 slice. The times are simulated.
32 devices in a mesh: replica: 8 (over z, x), shard: 4 (over y, core).
Axes of the slice: x: 2, y: 2, z: 4, core: 2. Of those that a mesh axis runs over, the one named last changes fastest.
Arguments:
- tokens_in: bfloat16 [32, 256, 2048], P(('replica', 'shard')), may hold values from -6 to 6
- cotangent: bfloat16 [32, 256, 2048], P(('replica', 'shard')), may hold values from -6 to 6
- segment_ids: int32 [32, 256], P(('replica', 'shard')), may hold values from 0 to 3, never falling along the last dimension, each value on 1 to 128 neighbouring positions
- attn_gain: bfloat16 [2048], P('shard'), may hold values from 0.5 to 1.5
- w_query: bfloat16 [2048, 1024], P('shard'), may hold values from -0.125 to 0.125
- w_key: bfloat16 [2048, 256], P('shard'), may hold values from -0.125 to 0.125
- w_value: bfloat16 [2048, 256], P('shard'), may hold values from -0.125 to 0.125
- w_output: bfloat16 [1024, 2048], P('shard'), may hold values from -1.5 to 1.5
- mlp_gain: bfloat16 [2048], P('shard'), may hold values from 0.5 to 1.5
- w_gate: bfloat16 [2048, 4096], P('shard'), may hold values from -0.125 to 0.125
- w_up: bfloat16 [2048, 4096], P('shard'), may hold values from -0.125 to 0.125
- w_down: bfloat16 [4096, 2048], P('shard'), may hold values from -0.09375 to 0.09375
Outputs:
- tokens_out: bfloat16 [32, 256, 2048], P(('replica', 'shard'))
- grad_tokens: bfloat16 [32, 256, 2048], P(('replica', 'shard'))
- grad_attn_gain: float32 [2048], P('shard')
- grad_query: float32 [2048, 1024], P('shard')
- grad_key: float32 [2048, 256], P('shard')
- grad_value: float32 [2048, 256], P('shard')
- grad_output: float32 [1024, 2048], P('shard')
- grad_mlp_gain: float32 [2048], P('shard')
- grad_gate: float32 [2048, 4096], P('shard')
- grad_up: float32 [2048, 4096], P('shard')
- grad_down: float32 [4096, 2048], P('shard')
Inputs may be any that keep to these rules, and one draw needn't show every extreme that they name: `segment_ids`: in each sequence segment numbers never fall, each segment holds 1 to 128 tokens, and some segment exactly that many.
All inputs are finite; a program needn't handle non-finite values.
Results may differ from a plain program's by a relative error of at most 0.02.
Values may be sent and summed in bfloat16 or wider, within the bound.
A program may use at most 384 MiB of HBM per device.

v0:
```python
import math
import jax
import jax.numpy as jnp
from jax import lax
from jax.sharding import PartitionSpec as P

KV = 4
HD = 64
epsilon = 1e-05
theta_base = 500000.0
neg_large = -1e30


def contract(form, left_arr, right_arr):
    return jnp.einsum(form, left_arr, right_arr, preferred_element_type=jnp.float32)


def matmul(left_arr, right_arr):
    return jnp.dot(left_arr, right_arr, preferred_element_type=jnp.float32)


def positions_of(segment_ids):
    column = lax.broadcasted_iota(jnp.int32, segment_ids.shape, 1)
    starts = jnp.concatenate(
        [
            jnp.ones_like(segment_ids[:, :1]),
            (segment_ids[:, 1:] != segment_ids[:, :-1]).astype(jnp.int32),
        ],
        axis=1,
    )
    seg_start = lax.cummax(jnp.where(starts > 0, column, jnp.zeros_like(column)), axis=1)
    return column - seg_start


def rotary_tables(segment_ids, head_dim):
    positions = positions_of(segment_ids).astype(jnp.float32)
    half_dim = head_dim // 2
    exponent = jnp.arange(half_dim).astype(jnp.float32) * (2.0 / head_dim)
    inverse = theta_base ** (-exponent)
    angles = positions[:, :, None] * inverse[None, None, :]
    return (jnp.cos(angles)[:, :, None, :], jnp.sin(angles)[:, :, None, :])


def rotate(field_in, cosine, sine_tab):
    half_dim = field_in.shape[-1] // 2
    front_half = field_in[..., :half_dim]
    back_half = field_in[..., half_dim:]
    return jnp.concatenate(
        [front_half * cosine - back_half * sine_tab, front_half * sine_tab + back_half * cosine],
        axis=-1,
    )


def rotate_back(field_in, cosine, sine_tab):
    half_dim = field_in.shape[-1] // 2
    front_half = field_in[..., :half_dim]
    back_half = field_in[..., half_dim:]
    return jnp.concatenate(
        [front_half * cosine + back_half * sine_tab, back_half * cosine - front_half * sine_tab],
        axis=-1,
    )


def mask_of(segment_ids):
    length = segment_ids.shape[1]
    same_doc = segment_ids[:, :, None] == segment_ids[:, None, :]
    row_idx = lax.broadcasted_iota(jnp.int32, (length, length), 0)
    col_idx = lax.broadcasted_iota(jnp.int32, (length, length), 1)
    return (same_doc & (row_idx >= col_idx)[None])[:, None, None, :, :]


def forward_pass(tokens_in, segment_ids, weights, head_dim, kv_heads):
    attn_gain, w_query, w_key, w_value, w_output, mlp_gain, w_gate, w_up, w_down = weights
    batches, length, model_width = tokens_in.shape
    query_heads = w_query.shape[1] // head_dim
    group_size = query_heads // kv_heads
    scaling = 1.0 / math.sqrt(head_dim)
    flat_in = tokens_in.reshape(batches * length, model_width).astype(jnp.float32)
    inv_attn = lax.rsqrt(jnp.mean(flat_in * flat_in, axis=1, keepdims=True) + epsilon)
    normed_one = (flat_in * inv_attn * attn_gain.astype(jnp.float32)).astype(jnp.bfloat16)
    cosine, sine_tab = rotary_tables(segment_ids, head_dim)
    query_raw = matmul(normed_one, w_query).reshape(batches, length, query_heads, head_dim)
    key_raw = matmul(normed_one, w_key).reshape(batches, length, kv_heads, head_dim)
    query_rot = (
        rotate(query_raw, cosine, sine_tab)
        .astype(jnp.bfloat16)
        .reshape(batches, length, kv_heads, group_size, head_dim)
    )
    key_rot = rotate(key_raw, cosine, sine_tab).astype(jnp.bfloat16)
    value_rows = (
        matmul(normed_one, w_value)
        .astype(jnp.bfloat16)
        .reshape(batches, length, kv_heads, head_dim)
    )
    attn_mask = mask_of(segment_ids)
    scores = jnp.where(
        attn_mask, contract("bqkgd,bskd->bkgqs", query_rot, key_rot) * scaling, neg_large
    )
    row_max = jnp.max(scores, axis=-1, keepdims=True)
    exp_scores = jnp.exp(scores - row_max)
    row_total = jnp.sum(exp_scores, axis=-1, keepdims=True)
    log_sum = row_max + jnp.log(row_total)
    attn_probs = (exp_scores / row_total).astype(jnp.bfloat16)
    context = (
        contract("bkgqs,bskd->bqkgd", attn_probs, value_rows)
        .astype(jnp.bfloat16)
        .reshape(batches * length, query_heads * head_dim)
    )
    hidden = flat_in + matmul(context, w_output)
    inv_mlp = lax.rsqrt(jnp.mean(hidden * hidden, axis=1, keepdims=True) + epsilon)
    normed_two = (hidden * inv_mlp * mlp_gain.astype(jnp.float32)).astype(jnp.bfloat16)
    gate_pre = matmul(normed_two, w_gate)
    up_pre = matmul(normed_two, w_up)
    activated = (jax.nn.silu(gate_pre) * up_pre).astype(jnp.bfloat16)
    tokens_out = (
        (hidden + matmul(activated, w_down))
        .astype(jnp.bfloat16)
        .reshape(batches, length, model_width)
    )
    stored = (
        flat_in,
        inv_attn,
        normed_one,
        query_rot,
        key_rot,
        value_rows,
        cosine,
        sine_tab,
        attn_mask,
        log_sum,
        context,
        hidden,
        inv_mlp,
        normed_two,
        gate_pre,
        up_pre,
        activated,
    )
    return (tokens_out, stored)


def backward_pass(cotangent, stored, weights, head_dim, kv_heads):
    attn_gain, w_query, w_key, w_value, w_output, mlp_gain, w_gate, w_up, w_down = weights
    (
        flat_in,
        inv_attn,
        normed_one,
        query_rot,
        key_rot,
        value_rows,
        cosine,
        sine_tab,
        attn_mask,
        log_sum,
        context,
        hidden,
        inv_mlp,
        normed_two,
        gate_pre,
        up_pre,
        activated,
    ) = stored
    batches, length, model_width = cotangent.shape
    query_heads = w_query.shape[1] // head_dim
    group_size = query_heads // kv_heads
    scaling = 1.0 / math.sqrt(head_dim)
    grad_out = cotangent.reshape(batches * length, model_width)
    grad_down = matmul(activated.T, grad_out)
    grad_act = matmul(grad_out, w_down.T)
    sigmoid_gate = jax.nn.sigmoid(gate_pre)
    silu_gate = gate_pre * sigmoid_gate
    grad_gate_pre = (
        grad_act * up_pre * sigmoid_gate * (1.0 + gate_pre * (1.0 - sigmoid_gate))
    ).astype(jnp.bfloat16)
    grad_up_pre = (grad_act * silu_gate).astype(jnp.bfloat16)
    grad_gate = matmul(normed_two.T, grad_gate_pre)
    grad_up = matmul(normed_two.T, grad_up_pre)
    grad_two = matmul(grad_gate_pre, w_gate.T) + matmul(grad_up_pre, w_up.T)
    grad_mlp_gain = jnp.sum(grad_two * hidden * inv_mlp, axis=0)
    scaled_two = grad_two * mlp_gain.astype(jnp.float32)
    grad_hidden = grad_out.astype(jnp.float32) + inv_mlp * (
        scaled_two
        - hidden * inv_mlp * inv_mlp * jnp.mean(scaled_two * hidden, axis=1, keepdims=True)
    )
    grad_hid_bf = grad_hidden.astype(jnp.bfloat16)
    grad_output = matmul(context.T, grad_hid_bf)
    grad_context = (
        matmul(grad_hid_bf, w_output.T)
        .astype(jnp.bfloat16)
        .reshape(batches, length, kv_heads, group_size, head_dim)
    )
    scores = jnp.where(
        attn_mask, contract("bqkgd,bskd->bkgqs", query_rot, key_rot) * scaling, neg_large
    )
    probs_full = jnp.exp(scores - log_sum)
    grad_value_rows = contract("bkgqs,bqkgd->bskd", probs_full.astype(jnp.bfloat16), grad_context)
    grad_probs = contract("bqkgd,bskd->bkgqs", grad_context, value_rows)
    context_five = context.reshape(batches, length, kv_heads, group_size, head_dim).astype(
        jnp.float32
    )
    row_dot = jnp.sum(grad_context.astype(jnp.float32) * context_five, axis=-1)
    row_dot = jnp.transpose(row_dot, (0, 2, 3, 1))[..., None]
    grad_scores = (probs_full * (grad_probs - row_dot) * scaling).astype(jnp.bfloat16)
    grad_q_rot = contract("bkgqs,bskd->bqkgd", grad_scores, key_rot).reshape(
        batches, length, query_heads, head_dim
    )
    grad_k_rot = contract("bkgqs,bqkgd->bskd", grad_scores, query_rot)
    grad_q_in = (
        rotate_back(grad_q_rot, cosine, sine_tab)
        .astype(jnp.bfloat16)
        .reshape(batches * length, query_heads * head_dim)
    )
    grad_k_in = (
        rotate_back(grad_k_rot, cosine, sine_tab)
        .astype(jnp.bfloat16)
        .reshape(batches * length, kv_heads * head_dim)
    )
    grad_v_in = grad_value_rows.astype(jnp.bfloat16).reshape(batches * length, kv_heads * head_dim)
    grad_query = matmul(normed_one.T, grad_q_in)
    grad_key = matmul(normed_one.T, grad_k_in)
    grad_value = matmul(normed_one.T, grad_v_in)
    grad_one = (
        matmul(grad_q_in, w_query.T) + matmul(grad_k_in, w_key.T) + matmul(grad_v_in, w_value.T)
    )
    grad_attn_gain = jnp.sum(grad_one * flat_in * inv_attn, axis=0)
    scaled_one = grad_one * attn_gain.astype(jnp.float32)
    grad_tokens = grad_hidden + inv_attn * (
        scaled_one
        - flat_in * inv_attn * inv_attn * jnp.mean(scaled_one * flat_in, axis=1, keepdims=True)
    )
    grad_tokens = grad_tokens.astype(jnp.bfloat16).reshape(batches, length, model_width)
    return (
        grad_tokens,
        (
            grad_attn_gain,
            grad_query,
            grad_key,
            grad_value,
            grad_output,
            grad_mlp_gain,
            grad_gate,
            grad_up,
            grad_down,
        ),
    )


def per_device(
    tokens_in,
    cotangent,
    segment_ids,
    attn_gain,
    w_query,
    w_key,
    w_value,
    w_output,
    mlp_gain,
    w_gate,
    w_up,
    w_down,
):
    gathered = (
        lax.all_gather(attn_gain, "shard", axis=0, tiled=True),
        lax.all_gather(w_query, "shard", axis=0, tiled=True),
        lax.all_gather(w_key, "shard", axis=0, tiled=True),
        lax.all_gather(w_value, "shard", axis=0, tiled=True),
        lax.all_gather(w_output, "shard", axis=0, tiled=True),
        lax.all_gather(mlp_gain, "shard", axis=0, tiled=True),
        lax.all_gather(w_gate, "shard", axis=0, tiled=True),
        lax.all_gather(w_up, "shard", axis=0, tiled=True),
        lax.all_gather(w_down, "shard", axis=0, tiled=True),
    )
    tokens_out, stored = forward_pass(tokens_in, segment_ids, gathered, HD, KV)
    regathered = (
        lax.all_gather(attn_gain, "shard", axis=0, tiled=True),
        lax.all_gather(w_query, "shard", axis=0, tiled=True),
        lax.all_gather(w_key, "shard", axis=0, tiled=True),
        lax.all_gather(w_value, "shard", axis=0, tiled=True),
        lax.all_gather(w_output, "shard", axis=0, tiled=True),
        lax.all_gather(mlp_gain, "shard", axis=0, tiled=True),
        lax.all_gather(w_gate, "shard", axis=0, tiled=True),
        lax.all_gather(w_up, "shard", axis=0, tiled=True),
        lax.all_gather(w_down, "shard", axis=0, tiled=True),
    )
    grad_tokens, grads = backward_pass(cotangent, stored, regathered, HD, KV)
    shares = (
        lax.psum_scatter(
            grads[0].astype(jnp.bfloat16), "shard", scatter_dimension=0, tiled=True
        ).astype(jnp.float32),
        lax.psum_scatter(
            grads[1].astype(jnp.bfloat16), "shard", scatter_dimension=0, tiled=True
        ).astype(jnp.float32),
        lax.psum_scatter(
            grads[2].astype(jnp.bfloat16), "shard", scatter_dimension=0, tiled=True
        ).astype(jnp.float32),
        lax.psum_scatter(
            grads[3].astype(jnp.bfloat16), "shard", scatter_dimension=0, tiled=True
        ).astype(jnp.float32),
        lax.psum_scatter(
            grads[4].astype(jnp.bfloat16), "shard", scatter_dimension=0, tiled=True
        ).astype(jnp.float32),
        lax.psum_scatter(
            grads[5].astype(jnp.bfloat16), "shard", scatter_dimension=0, tiled=True
        ).astype(jnp.float32),
        lax.psum_scatter(
            grads[6].astype(jnp.bfloat16), "shard", scatter_dimension=0, tiled=True
        ).astype(jnp.float32),
        lax.psum_scatter(
            grads[7].astype(jnp.bfloat16), "shard", scatter_dimension=0, tiled=True
        ).astype(jnp.float32),
        lax.psum_scatter(
            grads[8].astype(jnp.bfloat16), "shard", scatter_dimension=0, tiled=True
        ).astype(jnp.float32),
    )
    reduced = (
        lax.psum(shares[0].astype(jnp.bfloat16), "replica").astype(jnp.float32),
        lax.psum(shares[1].astype(jnp.bfloat16), "replica").astype(jnp.float32),
        lax.psum(shares[2].astype(jnp.bfloat16), "replica").astype(jnp.float32),
        lax.psum(shares[3].astype(jnp.bfloat16), "replica").astype(jnp.float32),
        lax.psum(shares[4].astype(jnp.bfloat16), "replica").astype(jnp.float32),
        lax.psum(shares[5].astype(jnp.bfloat16), "replica").astype(jnp.float32),
        lax.psum(shares[6].astype(jnp.bfloat16), "replica").astype(jnp.float32),
        lax.psum(shares[7].astype(jnp.bfloat16), "replica").astype(jnp.float32),
        lax.psum(shares[8].astype(jnp.bfloat16), "replica").astype(jnp.float32),
    )
    return (
        tokens_out,
        grad_tokens,
        reduced[0],
        reduced[1],
        reduced[2],
        reduced[3],
        reduced[4],
        reduced[5],
        reduced[6],
        reduced[7],
        reduced[8],
    )


def solution(mesh):
    placed = (
        P(("replica", "shard"), None, None),
        P(("replica", "shard"), None, None),
        P(("replica", "shard"), None),
        P("shard"),
        P("shard", None),
        P("shard", None),
        P("shard", None),
        P("shard", None),
        P("shard"),
        P("shard", None),
        P("shard", None),
        P("shard", None),
    )
    return jax.shard_map(
        per_device,
        mesh=mesh,
        in_specs=placed,
        out_specs=(
            P(("replica", "shard"), None, None),
            P(("replica", "shard"), None, None),
            P("shard"),
            P("shard", None),
            P("shard", None),
            P("shard", None),
            P("shard", None),
            P("shard"),
            P("shard", None),
            P("shard", None),
            P("shard", None),
        ),
        check_vma=False,
    )
```

profile of v0, /device:TPU:0, one launch (start us, length us, event | category | flops | bytes accessed | tf_op | source)
XLA Modules:
  0.0 1527.5 jit_solution(17978087372400527792)
XLA Ops:
  12.9 6.2 all-gather.1
  19.1 5.6 all-gather
  25.4 3.6 all-gather.12.cloned.1.call-done
  31.2 16.2 %all-gather.10.cloned.1.call-done = bf16[2048,256]{1,0:T(8,128)(2,1)} async-done(((bf16[512,256]{1,0:T(8,128)(2,1)}), bf16[2048,256]{1,0:T(8,128)(2,1)}) %all-gather.10.cloned.1.call-update) | async-done | bytes 1048592 | tf_op jit(solution)/shard_map/all_gather | solution.py:266
  47.3 1.9 convolution_convert_fusion.8
  49.2 34.2 %all-gather.14.cloned.1.call-done = bf16[2048,1024]{1,0:T(8,128)(2,1)} async-done(((bf16[512,1024]{1,0:T(8,128)(2,1)}), bf16[2048,1024]{1,0:T(8,128)(2,1)}) %all-gather.14.cloned.1.call-update) | async-done | bytes 4194320 | tf_op jit(solution)/shard_map/all_gather | solution.py:264
  83.4 6.6 copy.41
  90.0 3.9 convolution_bitcast_fusion
  97.0 2.0 fusion.39
  99.0 20.3 %all-gather.16.cloned.1.call-done = bf16[1024,2048]{1,0:T(8,128)(2,1)} async-done(((bf16[256,2048]{1,0:T(8,128)(2,1)}), bf16[1024,2048]{1,0:T(8,128)(2,1)}) %all-gather.16.cloned.1.call-update) | async-done | bytes 4194320 | tf_op jit(solution)/shard_map/all_gather | solution.py:267
  119.3 3.7 multiply_reduce_fusion.2
  125.0 101.6 %all-gather.20.cloned.1.call-done = bf16[2048,4096]{1,0:T(8,128)(2,1)} async-done(((bf16[512,4096]{1,0:T(8,128)(2,1)}), bf16[2048,4096]{1,0:T(8,128)(2,1)}) %all-gather.20.cloned.1.call-update) | async-done | bytes 16777232 | tf_op jit(solution)/shard_map/all_gather | solution.py:270
  226.6 13.0 fusion.84
  239.6 94.4 %all-gather.18.cloned.1.call-done = bf16[2048,4096]{1,0:T(8,128)(2,1)} async-done(((bf16[512,4096]{1,0:T(8,128)(2,1)}), bf16[2048,4096]{1,0:T(8,128)(2,1)}) %all-gather.18.cloned.1.call-update) | async-done | bytes 16777232 | tf_op jit(solution)/shard_map/all_gather | solution.py:269
  334.0 13.4 fusion.83
  347.4 94.1 %all-gather.22.cloned.1.call-done = bf16[4096,2048]{1,0:T(8,128)(2,1)} async-done(((bf16[1024,2048]{1,0:T(8,128)(2,1)}), bf16[4096,2048]{1,0:T(8,128)(2,1)}) %all-gather.22.cloned.1.call-update) | async-done | bytes 16777232 | tf_op jit(solution)/shard_map/all_gather | solution.py:271
  441.5 13.4 multiply_convert_fusion
  454.9 12.2 fusion.85
  467.1 13.8 multiply_reduce_fusion
  481.6 3.3 multiply_add_fusion
  485.3 2.1 convolution_convert_fusion.7
  487.4 2.0 copy.43
  489.5 3.3 fusion.48
  495.3 2.2 copy.44
  499.1 4.0 fusion.2
  506.9 4.3 convolution_convert_fusion.3
  512.1 2.1 fusion.31
  515.1 3.4 convolution_convert_fusion.4
  518.6 12.5 convolution_convert_fusion
  531.4 12.3 convolution_convert_fusion.1
  543.8 12.4 convolution_convert_fusion.2
  556.3 39.4 %reduce-scatter.14.cloned.1.call-done = bf16[256,2048]{1,0:T(8,128)(2,1)} async-done(((bf16[1024,2048]{1,0:T(8,128)(2,1)}), bf16[256,2048]{1,0:T(8,128)(2,1)}) %reduce-scatter.14.cloned.1.call-update) | async-done | bytes 1048592 | tf_op jit(solution)/shard_map/reduce_scatter | solution.py:299
  595.7 47.7 %reduce-scatter.8.cloned.1.call-done = bf16[512,1024]{1,0:T(8,128)(2,1)} async-done(((bf16[2048,1024]{1,0:T(8,128)(2,1)}), bf16[512,1024]{1,0:T(8,128)(2,1)}) %reduce-scatter.8.cloned.1.call-update) | async-done | bytes 1048592 | tf_op jit(solution)/shard_map/reduce_scatter | solution.py:290
  643.4 127.5 %reduce-scatter.20.cloned.1.call-done = bf16[1024,2048]{1,0:T(8,128)(2,1)} async-done(((bf16[4096,2048]{1,0:T(8,128)(2,1)}), bf16[1024,2048]{1,0:T(8,128)(2,1)}) %reduce-scatter.20.cloned.1.call-update) | async-done | bytes 4194320 | tf_op jit(solution)/shard_map/reduce_scatter | solution.py:311
  770.9 127.6 %reduce-scatter.18.cloned.1.call-done = bf16[512,4096]{1,0:T(8,128)(2,1)} async-done(((bf16[2048,4096]{1,0:T(8,128)(2,1)}), bf16[512,4096]{1,0:T(8,128)(2,1)}) %reduce-scatter.18.cloned.1.call-update) | async-done | bytes 4194320 | tf_op jit(solution)/shard_map/reduce_scatter | solution.py:308
  898.6 127.5 %reduce-scatter.16.cloned.1.call-done = bf16[512,4096]{1,0:T(8,128)(2,1)} async-done(((bf16[2048,4096]{1,0:T(8,128)(2,1)}), bf16[512,4096]{1,0:T(8,128)(2,1)}) %reduce-scatter.16.cloned.1.call-update) | async-done | bytes 4194320 | tf_op jit(solution)/shard_map/reduce_scatter | solution.py:305
  1028.0 3.7 fusion.86
  1033.0 2.2 fusion.25
  1035.2 5.9 all-reduce.4
  1041.2 23.3 %all-reduce.2 = (bf16[512]{0:T(512)(128)(2,1)S(1)}, bf16[512]{0:T(512)(128)(2,1)S(1)}) all-reduce(bf16[512]{0:T(512)(128)(2,1)S(1)} %dynamic-slice.1, bf16[512]{0:T(512)(128)(2,1)S(1)} %dynamic-slice.3), channel_id=1, replica_groups=mesh['replica'=8,'shard'=4] {'replica'}, use_global_device_ids=true, to_apply=%region_11.12 | all-reduce | flops 1024 | bytes 4096 | tf_op jit(solution)/shard_map/psum | solution.py:316
  1065.7 3.4 fusion.51
  1069.1 9.5 fusion.14
  1078.6 421.6 %all-reduce.7.cloned.1.call-done = (bf16[512,1024]{1,0:T(8,128)(2,1)}, bf16[512,256]{1,0:T(8,128)(2,1)}, bf16[512,256]{1,0:T(8,128)(2,1)}, bf16[256,2048]{1,0:T(...) async-done(((bf16[512,1024]{1,0:T(8,128)(2,1)}, bf16[512,256]{1,0:T(8,128)(2,1)}, bf16[512,256]{1,0:T(8,128)(2,1)}, ...) | async-done | bytes 15204368 | tf_op jit(solution)/shard_map/psum | solution.py:317
  1500.2 1.9 convert_element_type.289
  1502.1 1.9 convert_element_type.291
  1507.3 4.5 convert_element_type.297
  1511.8 4.5 convert_element_type.299
  1516.3 4.4 convert_element_type.301
  (149 shorter events, 31.6 us)
Async XLA Ops:
  7.2 21.9 %all-gather.12.cloned.1.call-start = ((), (), s32[]{:S(2)}) async-start(), calls=%async_computation.8 | async-start | bytes 1310720 | tf_op jit(solution)/shard_map/all_gather | solution.py:265
  7.9 39.4 %all-gather.10.cloned.1.call-start = ((), (), s32[]{:S(2)}) async-start(), calls=%async_computation.7 | async-start | bytes 1310720 | tf_op jit(solution)/shard_map/all_gather | solution.py:266
  8.7 74.7 %all-gather.14.cloned.1.call-start = ((), (), s32[]{:S(2)}) async-start(), calls=%async_computation.9 | async-start | bytes 5242880 | tf_op jit(solution)/shard_map/all_gather | solution.py:264
  9.4 109.9 %all-gather.16.cloned.1.call-start = ((), (), s32[]{:S(2)}) async-start(), calls=%async_computation.10 | async-start | bytes 5242880 | tf_op jit(solution)/shard_map/all_gather | solution.py:267
  10.0 216.7 %all-gather.20.cloned.1.call-start = ((), (), s32[]{:S(2)}) async-start(), calls=%async_computation.12 | async-start | bytes 20971520 | tf_op jit(solution)/shard_map/all_gather | solution.py:270
  10.6 323.4 %all-gather.18.cloned.1.call-start = ((), (), s32[]{:S(2)}) async-start(), calls=%async_computation.11 | async-start | bytes 20971520 | tf_op jit(solution)/shard_map/all_gather | solution.py:269
  11.1 0.8 copy-start.29
  11.1 1.7 copy-start.32
  11.2 1.7 copy-start.33
  11.2 13.5 copy-start
  11.2 430.3 %all-gather.22.cloned.1.call-start = ((), (), s32[]{:S(2)}) async-start(), calls=%async_computation.13 | async-start | bytes 20971520 | tf_op jit(solution)/shard_map/all_gather | solution.py:271
  11.9 544.3 %reduce-scatter.12.cloned.1.call-start = ((), (), s32[]{:S(2)}) async-start(), calls=%async_computation.16 | async-start | bytes 1310720 | tf_op jit(solution)/shard_map/reduce_scatter | solution.py:296
  25.0 65.0 %copy-start.27 = (f32[256]{0:T(256)}, f32[256]{0:T(256)S(1)}, u32[]{:S(2)}) copy-start(f32[256]{0:T(256)S(1)} %add_rsqrt_fusion.1) | copy-start | bytes 3076
  31.1 63.0 %copy-start.17 = (bf16[256,4,32]{0,2,1:T(8,128)(2,1)}, bf16[256,4,32]{0,2,1:T(8,128)(2,1)S(1)}, u32[]{:S(2)}) copy-start(bf16[256,4,32]{0,2,1:T(8,128)(2,1)S(1)} %get-tuple-element.35) | copy-start | bytes 196612
  31.2 63.0 %copy-start.19 = (bf16[256,4,32]{0,2,1:T(8,128)(2,1)}, bf16[256,4,32]{0,2,1:T(8,128)(2,1)S(1)}, u32[]{:S(2)}) copy-start(bf16[256,4,32]{0,2,1:T(8,128)(2,1)S(1)} %get-tuple-element.36) | copy-start | bytes 196612
  49.2 46.6 %copy-start.34 = (bf16[256,256]{0,1:T(8,128)(2,1)}, bf16[256,256]{0,1:T(8,128)(2,1)S(1)}, u32[]{:S(2)}) copy-start(bf16[256,256]{0,1:T(8,128)(2,1)S(1)} %convolution_convert_fusion.8) | copy-start | bytes 393220
  94.1 0.8 copy-start.15
  94.9 2.0 copy-start.8
  95.0 2.0 copy-start.23
  95.9 3.1 copy-start.25
  119.3 3.8 copy-start.24
  119.3 3.8 copy-start.26
  123.0 344.1 %copy-start.1 = (f32[256,2048]{1,0:T(8,128)}, f32[256,2048]{1,0:T(8,128)S(1)}, u32[]{:S(2)}) copy-start(f32[256,2048]{1,0:T(8,128)S(1)} %get-tuple-element.42) | copy-start | bytes 6291460
  481.6 3.8 copy-start.3
  489.5 4.0 copy-start.28
  495.3 61.0 %reduce-scatter.10.cloned.1.call-start = ((), (), s32[]{:S(2)}) async-start(), calls=%async_computation.15 | async-start | bytes 1310720 | tf_op jit(solution)/shard_map/reduce_scatter | solution.py:293
  499.1 5.3 copy-start.16
  503.1 1.3 copy-start.4
  506.8 88.8 %reduce-scatter.14.cloned.1.call-start = ((), (), s32[]{:S(2)}) async-start(), calls=%async_computation.17 | async-start | bytes 5242880 | tf_op jit(solution)/shard_map/reduce_scatter | solution.py:299
  511.2 0.8 copy-start.18
  511.2 0.9 copy-start.20
  511.2 132.2 %reduce-scatter.8.cloned.1.call-start = ((), (), s32[]{:S(2)}) async-start(), calls=%async_computation.14 | async-start | bytes 5242880 | tf_op jit(solution)/shard_map/reduce_scatter | solution.py:290
  514.3 0.8 copy-start.11
  518.6 252.3 %reduce-scatter.20.cloned.1.call-start = ((), (), s32[]{:S(2)}) async-start(), calls=%async_computation.20 | async-start | bytes 20971520 | tf_op jit(solution)/shard_map/reduce_scatter | solution.py:311
  531.2 367.4 %reduce-scatter.18.cloned.1.call-start = ((), (), s32[]{:S(2)}) async-start(), calls=%async_computation.19 | async-start | bytes 20971520 | tf_op jit(solution)/shard_map/reduce_scatter | solution.py:308
  543.7 482.3 %reduce-scatter.16.cloned.1.call-start = ((), (), s32[]{:S(2)}) async-start(), calls=%async_computation.18 | async-start | bytes 20971520 | tf_op jit(solution)/shard_map/reduce_scatter | solution.py:305
  556.2 944.0 %all-reduce.7.cloned.1.call-start = ((), (), s32[]{:S(2)}) async-start(), calls=%async_computation.21 | async-start | bytes 30408704 | tf_op jit(solution)/shard_map/psum | solution.py:317
  1028.0 3.8 copy-start.9
  1031.7 1.2 copy-start.14
  1031.7 1.2 copy-start.22
  1033.0 2.2 copy-start.31
  1065.7 3.4 copy-start.2
  1065.7 3.4 copy-start.10
  1500.2 3.7 copy-start.13
  1502.1 3.4 copy-start.12
  1503.9 3.4 copy-start.7
  1507.3 4.5 copy-start.6
  1511.8 4.5 copy-start.5
  (3 other events, 2.1 us)
Sparse Core Ops, SparseCore 0:
  9.5 19.4 all-gather.11
  30.6 16.6 all-gather.9
  48.9 34.4 all-gather.13
  84.8 34.4 all-gather.15
  120.7 105.8 all-gather.19
  228.0 105.8 all-gather.17
  335.5 105.8 all-gather.21
  495.4 24.7 reduce-scatter.11
  523.3 24.7 reduce-scatter.9
  551.1 44.5 reduce-scatter.13
  598.8 44.5 reduce-scatter.7
  645.8 125.0 reduce-scatter.19
  773.5 125.0 reduce-scatter.17
  901.0 125.0 reduce-scatter.15
  1031.7 468.4 all-reduce.6
where the time goes:
time: 1530 us
  waiting for transfers between devices  1260 us (82%)
  matrix products  155 us (10%)
  blocking collectives  40.9 us (3%)
  other arithmetic  34.8 us (2%)
  local copies, waits for them, and re-layouts  20.1 us (1%)
  between operations  15.4 us (1%)
    psum x1, waiting for transfers between devices, per_device(): lax.psum(shares[1].astype(jnp.bfloat16), 'replica').astype(jnp.float32)  422 us
    dot_general x21, matrix products, matmul(): return jnp.dot(left_arr, right_arr, preferred_element_type=jnp.float32)  142 us
    reduce_scatter x1, waiting for transfers between devices, per_device(): lax.psum_scatter(grads[7].astype(jnp.bfloat16), 'shard', scatter_dimensio...  128 us
    reduce_scatter x1, waiting for transfers between devices, per_device(): lax.psum_scatter(grads[8].astype(jnp.bfloat16), 'shard', scatter_dimensio...  128 us
    reduce_scatter x1, waiting for transfers between devices, per_device(): lax.psum_scatter(grads[6].astype(jnp.bfloat16), 'shard', scatter_dimensio...  128 us
    all_gather x1, waiting for transfers between devices, per_device(): lax.all_gather(w_up, 'shard', axis=0, tiled=True)  102 us
    all_gather x1, waiting for transfers between devices, per_device(): lax.all_gather(w_gate, 'shard', axis=0, tiled=True)  94.4 us
    all_gather x1, waiting for transfers between devices, per_device(): lax.all_gather(w_down, 'shard', axis=0, tiled=True)  94.1 us
  transfers between devices with their start and end apart: 15, of which 13 were waited for; matrix products, arithmetic and copies ran while one was open for 9% of the time, Pallas kernels for 0%

commit v1 on v0

--- a/solution.py
+++ b/solution.py
@@ -9,6 +9,11 @@
 epsilon = 1e-05
 theta_base = 500000.0
 neg_large = -1e30
+
+
+def add_all(array, axis):
+    parts = lax.all_gather(array, axis)
+    return jnp.sum(parts, axis=0)
 
 
 def contract(form, left_arr, right_arr):
@@ -314,7 +319,7 @@
     )
     reduced = (
         lax.psum(shares[0].astype(jnp.bfloat16), "replica").astype(jnp.float32),
-        lax.psum(shares[1].astype(jnp.bfloat16), "replica").astype(jnp.float32),
+        add_all(shares[1].astype(jnp.bfloat16), "replica").astype(jnp.float32),
         lax.psum(shares[2].astype(jnp.bfloat16), "replica").astype(jnp.float32),
         lax.psum(shares[3].astype(jnp.bfloat16), "replica").astype(jnp.float32),
         lax.psum(shares[4].astype(jnp.bfloat16), "replica").astype(jnp.float32),

time: 1530 us -> 1630 us (1.065)
  waiting for transfers between devices: 1260 us -> 1360 us
    all_gather x0 -> x1, waiting for transfers between devices: none -> 74.8 us  [add_all(): parts = lax.all_gather(array, axis)]
    reduce_scatter x1, waiting for transfers between devices: 47.7 us -> 0.02 us  [per_device(): lax.psum_scatter(grads[1].astype(jnp.bfloat16), 'shard', scatter_dimensio...]
    reduce_scatter x1, waiting for transfers between devices: 0.02 us -> 27.7 us  [per_device(): lax.psum_scatter(grads[2].astype(jnp.bfloat16), 'shard', scatter_dimensio...]
    reduce_scatter x1, waiting for transfers between devices: 0.02 us -> 20.7 us  [per_device(): lax.psum_scatter(grads[3].astype(jnp.bfloat16), 'shard', scatter_dimensio...]
  transfers between devices with their start and end apart: 15 -> 16, of which waited for: 13 -> 15; matrix products, arithmetic and copies ran while one was open for 9% -> 8% of each run, Pallas kernels for 0% -> 0%
where the time goes in v1:
time: 1630 us
  waiting for transfers between devices  1360 us (83%)
  matrix products  154 us (9%)
  other arithmetic  41.7 us (3%)
  blocking collectives  40.6 us (2%)
  local copies, waits for them, and re-layouts  18.4 us (1%)
    psum x1, waiting for transfers between devices, per_device(): lax.psum(shares[2].astype(jnp.bfloat16), 'replica').astype(jnp.float32)  433 us
    dot_general x21, matrix products, matmul(): return jnp.dot(left_arr, right_arr, preferred_element_type=jnp.float32)  141 us
    reduce_scatter x1, waiting for transfers between devices, per_device(): lax.psum_scatter(grads[7].astype(jnp.bfloat16), 'shard', scatter_dimensio...  128 us
    reduce_scatter x1, waiting for transfers between devices, per_device(): lax.psum_scatter(grads[8].astype(jnp.bfloat16), 'shard', scatter_dimensio...  128 us
    reduce_scatter x1, waiting for transfers between devices, per_device(): lax.psum_scatter(grads[6].astype(jnp.bfloat16), 'shard', scatter_dimensio...  128 us
    all_gather x1, waiting for transfers between devices, per_device(): lax.all_gather(w_up, 'shard', axis=0, tiled=True)  102 us
    all_gather x1, waiting for transfers between devices, per_device(): lax.all_gather(w_gate, 'shard', axis=0, tiled=True)  94.4 us
    all_gather x1, waiting for transfers between devices, per_device(): lax.all_gather(w_down, 'shard', axis=0, tiled=True)  94.1 us
  transfers between devices with their start and end apart: 16, of which 15 were waited for; matrix products, arithmetic and copies ran while one was open for 8% of the time, Pallas kernels for 0%

profile of v1, /device:TPU:0, one launch (start us, length us, event | category | flops | bytes accessed | tf_op | source)
XLA Modules:
  0.0 1627.4 jit_solution(2525651051474912317)
XLA Ops:
  12.9 6.2 all-gather.2
  19.1 5.6 all-gather.1
  25.4 3.6 all-gather.14.cloned.1.call-done
  31.2 16.2 all-gather.12.cloned.1.call-done
  49.2 34.2 %all-gather.16.cloned.1.call-done = bf16[2048,1024]{1,0:T(8,128)(2,1)} async-done(((bf16[512,1024]{1,0:T(8,128)(2,1)}), bf16[2048,1024]{1,0:T(8,128)(2,1)}) %all-gather.16.cloned.1.call-update) | async-done | bytes 4194320 | tf_op jit(solution)/shard_map/all_gather | solution.py:269
  83.4 6.6 copy.41
  90.0 3.9 convolution_bitcast_fusion
  99.0 20.3 %all-gather.18.cloned.1.call-done = bf16[1024,2048]{1,0:T(8,128)(2,1)} async-done(((bf16[256,2048]{1,0:T(8,128)(2,1)}), bf16[1024,2048]{1,0:T(8,128)(2,1)}) %all-gather.18.cloned.1.call-update) | async-done | bytes 4194320 | tf_op jit(solution)/shard_map/all_gather | solution.py:272
  119.3 3.7 multiply_reduce_fusion.2
  125.0 101.6 %all-gather.22.cloned.1.call-done = bf16[2048,4096]{1,0:T(8,128)(2,1)} async-done(((bf16[512,4096]{1,0:T(8,128)(2,1)}), bf16[2048,4096]{1,0:T(8,128)(2,1)}) %all-gather.22.cloned.1.call-update) | async-done | bytes 16777232 | tf_op jit(solution)/shard_map/all_gather | solution.py:275
  226.6 13.0 fusion.84
  239.6 94.4 %all-gather.20.cloned.1.call-done = bf16[2048,4096]{1,0:T(8,128)(2,1)} async-done(((bf16[512,4096]{1,0:T(8,128)(2,1)}), bf16[2048,4096]{1,0:T(8,128)(2,1)}) %all-gather.20.cloned.1.call-update) | async-done | bytes 16777232 | tf_op jit(solution)/shard_map/all_gather | solution.py:274
  334.0 13.4 fusion.83
  347.4 94.1 %all-gather.24.cloned.1.call-done = bf16[4096,2048]{1,0:T(8,128)(2,1)} async-done(((bf16[1024,2048]{1,0:T(8,128)(2,1)}), bf16[4096,2048]{1,0:T(8,128)(2,1)}) %all-gather.24.cloned.1.call-update) | async-done | bytes 16777232 | tf_op jit(solution)/shard_map/all_gather | solution.py:276
  441.5 13.3 multiply_convert_fusion
  454.8 12.2 fusion.85
  467.0 13.8 multiply_reduce_fusion
  481.5 3.3 multiply_add_fusion
  485.3 2.1 convolution_convert_fusion.7
  487.3 2.0 copy.43
  489.4 2.2 copy.44
  493.1 4.0 fusion.2
  499.3 3.4 convolution_convert_fusion.4
  502.8 3.3 fusion.48
  508.4 2.5 fusion.45
  512.6 4.3 convolution_convert_fusion.3
  517.1 12.2 convolution_convert_fusion
  529.5 12.3 convolution_convert_fusion.1
  541.9 12.2 convolution_convert_fusion.2
  554.8 20.7 %reduce-scatter.12.cloned.1.call-done = bf16[512,256]{1,0:T(8,128)(2,1)} async-done(((bf16[2048,256]{1,0:T(8,128)(2,1)}), bf16[512,256]{1,0:T(8,128)(2,1)}) %reduce-scatter.12.cloned.1.call-update) | async-done | bytes 262160 | tf_op jit(solution)/shard_map/reduce_scatter | solution.py:301
  575.4 27.7 %reduce-scatter.10.cloned.1.call-done = bf16[512,256]{1,0:T(8,128)(2,1)} async-done(((bf16[2048,256]{1,0:T(8,128)(2,1)}), bf16[512,256]{1,0:T(8,128)(2,1)}) %reduce-scatter.10.cloned.1.call-update) | async-done | bytes 262160 | tf_op jit(solution)/shard_map/reduce_scatter | solution.py:298
  603.2 47.7 %reduce-scatter.14.cloned.1.call-done = bf16[256,2048]{1,0:T(8,128)(2,1)} async-done(((bf16[1024,2048]{1,0:T(8,128)(2,1)}), bf16[256,2048]{1,0:T(8,128)(2,1)}) %reduce-scatter.14.cloned.1.call-update) | async-done | bytes 1048592 | tf_op jit(solution)/shard_map/reduce_scatter | solution.py:304
  650.8 127.5 %reduce-scatter.20.cloned.1.call-done = bf16[1024,2048]{1,0:T(8,128)(2,1)} async-done(((bf16[4096,2048]{1,0:T(8,128)(2,1)}), bf16[1024,2048]{1,0:T(8,128)(2,1)}) %reduce-scatter.20.cloned.1.call-update) | async-done | bytes 4194320 | tf_op jit(solution)/shard_map/reduce_scatter | solution.py:316
  778.4 127.7 %reduce-scatter.18.cloned.1.call-done = bf16[512,4096]{1,0:T(8,128)(2,1)} async-done(((bf16[2048,4096]{1,0:T(8,128)(2,1)}), bf16[512,4096]{1,0:T(8,128)(2,1)}) %reduce-scatter.18.cloned.1.call-update) | async-done | bytes 4194320 | tf_op jit(solution)/shard_map/reduce_scatter | solution.py:313
  906.0 127.5 %reduce-scatter.16.cloned.1.call-done = bf16[512,4096]{1,0:T(8,128)(2,1)} async-done(((bf16[2048,4096]{1,0:T(8,128)(2,1)}), bf16[512,4096]{1,0:T(8,128)(2,1)}) %reduce-scatter.16.cloned.1.call-update) | async-done | bytes 4194320 | tf_op jit(solution)/shard_map/reduce_scatter | solution.py:310
  1035.5 3.7 fusion.86
  1040.4 2.2 fusion.25
  1042.7 5.9 all-reduce.4
  1048.7 23.0 %all-reduce.2 = (bf16[512]{0:T(512)(128)(2,1)S(1)}, bf16[512]{0:T(512)(128)(2,1)S(1)}) all-reduce(bf16[512]{0:T(512)(128)(2,1)S(1)} %dynamic-slice.1, bf16[512]{0:T(512)(128)(2,1)S(1)} %dynamic-slice.3), channel_id=1, replica_groups=mesh['replica'=8,'shard'=4] {'replica'}, use_global_device_ids=true, to_apply=%region_11.12 | all-reduce | flops 1024 | bytes 4096 | tf_op jit(solution)/shard_map/psum | solution.py:321
  1072.9 3.4 fusion.51
  1076.2 9.3 fusion.14
  1085.6 74.8 %all-gather.26.cloned.1.call-done = bf16[4096,1024]{1,0:T(8,128)(2,1)} async-done(((bf16[512,1024]{1,0:T(8,128)(2,1)}), bf16[4096,1024]{1,0:T(8,128)(2,1)}) %all-gather.26.cloned.1.call-update) | async-done | bytes 8388624 | tf_op jit(solution)/shard_map/all_gather | solution.py:15
  1160.4 5.7 reduce_sum.94
  1167.6 433.1 %all-reduce.7.cloned.1.call-done = (bf16[512,256]{1,0:T(8,128)(2,1)}, bf16[512,256]{1,0:T(8,128)(2,1)}, bf16[256,2048]{1,0:T(8,128)(2,1)}, bf16[512,4096]{1,0:T(...) async-done(((bf16[512,256]{1,0:T(8,128)(2,1)}, bf16[512,256]{1,0:T(8,128)(2,1)}, bf16[256,2048]{1,0:T(8,128)(2,1)}, bf16[512,4096]{1,0:T(8,128)(2,1)}, ...) | async-done | bytes 14155792 | tf_op jit(solution)/shard_map/psum | solution.py:323
  1604.4 2.8 convert_element_type.295
  1607.2 4.5 convert_element_type.299
  1611.7 4.5 convert_element_type.301
  1616.2 4.4 convert_element_type.303
  (147 shorter events, 36.0 us)
Async XLA Ops:
  7.2 21.9 %all-gather.14.cloned.1.call-start = ((), (), s32[]{:S(2)}) async-start(), calls=%async_computation.8 | async-start | bytes 1310720 | tf_op jit(solution)/shard_map/all_gather | solution.py:270
  7.9 39.4 %all-gather.12.cloned.1.call-start = ((), (), s32[]{:S(2)}) async-start(), calls=%async_computation.7 | async-start | bytes 1310720 | tf_op jit(solution)/shard_map/all_gather | solution.py:271
  8.7 74.7 %all-gather.16.cloned.1.call-start = ((), (), s32[]{:S(2)}) async-start(), calls=%async_computation.9 | async-start | bytes 5242880 | tf_op jit(solution)/shard_map/all_gather | solution.py:269
  9.4 109.9 %all-gather.18.cloned.1.call-start = ((), (), s32[]{:S(2)}) async-start(), calls=%async_computation.10 | async-start | bytes 5242880 | tf_op jit(solution)/shard_map/all_gather | solution.py:272
  10.0 216.7 %all-gather.22.cloned.1.call-start = ((), (), s32[]{:S(2)}) async-start(), calls=%async_computation.12 | async-start | bytes 20971520 | tf_op jit(solution)/shard_map/all_gather | solution.py:275
  10.6 323.4 %all-gather.20.cloned.1.call-start = ((), (), s32[]{:S(2)}) async-start(), calls=%async_computation.11 | async-start | bytes 20971520 | tf_op jit(solution)/shard_map/all_gather | solution.py:274
  11.1 0.8 copy-start.26
  11.1 1.7 copy-start.29
  11.2 1.7 copy-start.30
  11.2 13.5 copy-start
  11.2 430.3 %all-gather.24.cloned.1.call-start = ((), (), s32[]{:S(2)}) async-start(), calls=%async_computation.13 | async-start | bytes 20971520 | tf_op jit(solution)/shard_map/all_gather | solution.py:276
  11.9 542.3 %reduce-scatter.8.cloned.1.call-start = ((), (), s32[]{:S(2)}) async-start(), calls=%async_computation.14 | async-start | bytes 5242880 | tf_op jit(solution)/shard_map/reduce_scatter | solution.py:295
  25.0 65.0 %copy-start.24 = (f32[256]{0:T(256)}, f32[256]{0:T(256)S(1)}, u32[]{:S(2)}) copy-start(f32[256]{0:T(256)S(1)} %add_rsqrt_fusion.1) | copy-start | bytes 3076
  31.1 63.0 %copy-start.14 = (bf16[256,4,32]{0,2,1:T(8,128)(2,1)}, bf16[256,4,32]{0,2,1:T(8,128)(2,1)S(1)}, u32[]{:S(2)}) copy-start(bf16[256,4,32]{0,2,1:T(8,128)(2,1)S(1)} %get-tuple-element.34) | copy-start | bytes 196612
  31.2 63.0 %copy-start.16 = (bf16[256,4,32]{0,2,1:T(8,128)(2,1)}, bf16[256,4,32]{0,2,1:T(8,128)(2,1)S(1)}, u32[]{:S(2)}) copy-start(bf16[256,4,32]{0,2,1:T(8,128)(2,1)S(1)} %get-tuple-element.35) | copy-start | bytes 196612
  49.2 46.7 %copy-start.31 = (bf16[256,256]{0,1:T(8,128)(2,1)}, bf16[256,256]{0,1:T(8,128)(2,1)S(1)}, u32[]{:S(2)}) copy-start(bf16[256,256]{0,1:T(8,128)(2,1)S(1)} %convolution_convert_fusion.8) | copy-start | bytes 393220
  94.1 0.8 copy-start.13
  94.9 2.0 copy-start.8
  95.0 2.0 copy-start.20
  95.9 3.1 copy-start.22
  119.3 3.8 copy-start.21
  119.3 3.8 copy-start.23
  123.0 344.0 %copy-start.1 = (f32[256,2048]{1,0:T(8,128)}, f32[256,2048]{1,0:T(8,128)S(1)}, u32[]{:S(2)}) copy-start(f32[256,2048]{1,0:T(8,128)S(1)} %get-tuple-element.41) | copy-start | bytes 6291460
  123.1 0.7 copy-start.27
  481.5 3.8 copy-start.3
  493.1 4.0 copy-start.15
  493.1 4.0 copy-start.17
  497.2 1.3 copy-start.4
  497.6 1.7 copy-start.25
  498.5 0.8 copy-start.11
  502.8 72.7 %reduce-scatter.12.cloned.1.call-start = ((), (), s32[]{:S(2)}) async-start(), calls=%async_computation.16 | async-start | bytes 1310720 | tf_op jit(solution)/shard_map/reduce_scatter | solution.py:301
  508.4 94.8 %reduce-scatter.10.cloned.1.call-start = ((), (), s32[]{:S(2)}) async-start(), calls=%async_computation.15 | async-start | bytes 1310720 | tf_op jit(solution)/shard_map/reduce_scatter | solution.py:298
  512.6 138.2 %reduce-scatter.14.cloned.1.call-start = ((), (), s32[]{:S(2)}) async-start(), calls=%async_computation.17 | async-start | bytes 5242880 | tf_op jit(solution)/shard_map/reduce_scatter | solution.py:304
  517.0 261.4 %reduce-scatter.20.cloned.1.call-start = ((), (), s32[]{:S(2)}) async-start(), calls=%async_computation.20 | async-start | bytes 20971520 | tf_op jit(solution)/shard_map/reduce_scatter | solution.py:316
  529.3 376.8 %reduce-scatter.18.cloned.1.call-start = ((), (), s32[]{:S(2)}) async-start(), calls=%async_computation.19 | async-start | bytes 20971520 | tf_op jit(solution)/shard_map/reduce_scatter | solution.py:313
  541.8 491.7 %reduce-scatter.16.cloned.1.call-start = ((), (), s32[]{:S(2)}) async-start(), calls=%async_computation.18 | async-start | bytes 20971520 | tf_op jit(solution)/shard_map/reduce_scatter | solution.py:310
  554.1 606.3 %all-gather.26.cloned.1.call-start = ((), (), s32[]{:S(2)}) async-start(), calls=%async_computation.21 | async-start | bytes 9437184 | tf_op jit(solution)/shard_map/all_gather | solution.py:15
  554.7 1046.0 %all-reduce.7.cloned.1.call-start = ((), (), s32[]{:S(2)}) async-start(), calls=%async_computation.22 | async-start | bytes 28311552 | tf_op jit(solution)/shard_map/psum | solution.py:323
  1033.6 0.7 copy-start.32
  1035.4 3.8 copy-start.9
  1039.2 1.2 copy-start.12
  1039.2 1.2 copy-start.19
  1040.4 2.2 copy-start.28
  1072.9 3.4 copy-start.2
  1072.9 3.4 copy-start.10
  1600.7 6.5 copy-start.7
  1607.2 4.5 copy-start.6
  1611.7 4.5 copy-start.5
  (1 other events, 0.7 us)
Sparse Core Ops, SparseCore 0:
  9.5 19.4 all-gather.13
  30.6 16.6 all-gather.11
  48.9 34.4 all-gather.15
  84.8 34.4 all-gather.17
  120.7 105.8 all-gather.21
  228.0 105.8 all-gather.19
  335.5 105.8 all-gather.23
  502.9 44.5 reduce-scatter.7
  550.6 24.7 reduce-scatter.11
  578.4 24.7 reduce-scatter.9
  606.3 44.5 reduce-scatter.13
  653.3 125.0 reduce-scatter.19
  781.0 125.0 reduce-scatter.17
  908.5 125.0 reduce-scatter.15
  1035.5 124.8 all-gather.25
  1165.7 434.9 all-reduce.6
